TPU v7x, 32 devices: a whole 2x2x4 slice. The times are simulated.
32 devices in a mesh: dp: 8 (over y, x, core), fsdp: 4 (over z).
Axes of the slice: x: 2, y: 2, z: 4, core: 2. Of those that a mesh axis runs over, the one named last changes fastest.
Arguments:
- tokens: bfloat16 [64, 512, 768], P(('dp', 'fsdp')), may hold values from -6 to 6
- lengths: int32 [64], P(('dp', 'fsdp')), may hold values from 1 to 512, 24576 in all
- cotangent: bfloat16 [64, 512, 768], P(('dp', 'fsdp')), may hold values from -6 to 6
- w_query: bfloat16 [768, 768], P(('dp', 'fsdp')), may hold values from -0.21875 to 0.21875
- w_key: bfloat16 [768, 768], P(('dp', 'fsdp')), may hold values from -0.21875 to 0.21875
- w_value: bfloat16 [768, 768], P(('dp', 'fsdp')), may hold values from -0.21875 to 0.21875
- w_out: bfloat16 [768, 768], P(('dp', 'fsdp')), may hold values from -0.875 to 0.875
- w_up: bfloat16 [768, 3072], P(('dp', 'fsdp')), may hold values from -0.21875 to 0.21875
- w_down: bfloat16 [3072, 768], P(('dp', 'fsdp')), may hold values from -0.109375 to 0.109375
- shared_a: bfloat16 [768, 1024], P(('dp', 'fsdp')), may hold values from -0.21875 to 0.21875
- shared_b: bfloat16 [1024, 768], P(('dp', 'fsdp')), may hold values from -0.1875 to 0.1875
- gain_one: float32 [768], replicated, may hold values from 0.5 to 1.5
- gain_two: float32 [768], replicated, may hold values from 0.5 to 1.5
- query_d: float32 [1024], replicated, may hold values from -4 to 4
- query_b: float32 [768], replicated, may hold values from -4 to 4
- value_d: float32 [1024], replicated, may hold values from -4 to 4
- value_b: float32 [768], replicated, may hold values from -4 to 4
Outputs:
- output: bfloat16 [64, 512, 768], P(('dp', 'fsdp'))
- grad_tokens: bfloat16 [64, 512, 768], P(('dp', 'fsdp'))
- grad_query_d: float32 [1024], replicated
- grad_query_b: float32 [768], replicated
- grad_value_d: float32 [1024], replicated
- grad_value_b: float32 [768], replicated
- rank_stats: float32 [1024], replicated
Inputs may be any that keep to these rules, and one draw needn't show every extreme that they name: The 64 lengths sum to 24576, and the largest equals 512.
All inputs are finite; a program needn't handle non-finite values. No bound on the sum of `lengths` on one device may be relied on, other than what follows from the above.
Results may differ from a plain program's by a relative error of at most 0.015.
The roundings to bfloat16 on the way count: a program that leaves them out, or rounds other values in their place, can miss the bound.
Values may be sent and summed in bfloat16 or wider, within the bound.
A program may use at most 192 MiB of HBM per device.

v0:
```python
import jax
import jax.numpy as jnp
from jax import lax
from jax.sharding import PartitionSpec as P

D = 768
H = 12
HD = 64
L = 512
SEQ_DEV = 2
eps_norm = 1e-05
neg_fill = -1000000000.0


def layer_norm(hidden, gain):
    center = jnp.mean(hidden, axis=-1, keepdims=True)
    shifted = hidden - center
    spread = jnp.mean(shifted * shifted, axis=-1, keepdims=True)
    return shifted * lax.rsqrt(spread + eps_norm) * gain


def exact_gelu(pre_act):
    return jax.nn.gelu(pre_act, approximate=False)


def dot_plain(left, right):
    return jnp.dot(left, right, preferred_element_type=jnp.float32)


def dot_trans(left, right):
    return lax.dot_general(
        left, right, (((1,), (1,)), ((), ())), preferred_element_type=jnp.float32
    )


def split_heads(row_data):
    return row_data.reshape(SEQ_DEV, L, H, HD).transpose(0, 2, 1, 3).reshape(SEQ_DEV * H, L, HD)


def join_heads(head_data):
    return head_data.reshape(SEQ_DEV, H, L, HD).transpose(0, 2, 1, 3).reshape(SEQ_DEV * L, D)


def shards(
    tokens,
    lengths,
    cotangent,
    w_query,
    w_key,
    w_value,
    w_out,
    w_up,
    w_down,
    shared_a,
    shared_b,
    gain_one,
    gain_two,
    query_d,
    query_b,
    value_d,
    value_b,
):
    row_count = SEQ_DEV * L
    head_scale = HD ** (-0.5)
    local_mats = (w_query, w_key, w_value, w_out, w_up, w_down, shared_a, shared_b)
    full_mats = (
        lax.all_gather(local_mats[0], ("dp", "fsdp"), axis=0, tiled=True),
        lax.all_gather(local_mats[1], ("dp", "fsdp"), axis=0, tiled=True),
        lax.all_gather(local_mats[2], ("dp", "fsdp"), axis=0, tiled=True),
        lax.all_gather(local_mats[3], ("dp", "fsdp"), axis=0, tiled=True),
        lax.all_gather(local_mats[4], ("dp", "fsdp"), axis=0, tiled=True),
        lax.all_gather(local_mats[5], ("dp", "fsdp"), axis=0, tiled=True),
        lax.all_gather(local_mats[6], ("dp", "fsdp"), axis=0, tiled=True),
        lax.all_gather(local_mats[7], ("dp", "fsdp"), axis=0, tiled=True),
    )
    wq, wk, wv, wo, wu, wd, mat_a, mat_b = full_mats
    inputs = tokens.reshape(row_count, D)
    positions = lax.broadcasted_iota(jnp.int32, (SEQ_DEV, L), 1)
    live = (positions < lengths[:, None]).astype(jnp.float32)
    live_rows = live.reshape(row_count, 1)
    key_live = jnp.repeat(live, H, axis=0)
    rank_act = dot_plain(inputs, mat_a)
    square_sum = jnp.sum(rank_act * rank_act * live_rows, axis=0)
    count = jnp.sum(lengths).astype(jnp.float32)
    total_square, total_count = lax.psum((square_sum, count), ("dp", "fsdp"))
    rank_q = (rank_act * query_d).astype(jnp.bfloat16)
    rank_v = (rank_act * value_d).astype(jnp.bfloat16)
    delta_q = dot_plain(rank_q, mat_b)
    delta_v = dot_plain(rank_v, mat_b)
    queries = (dot_plain(inputs, wq) + query_b * delta_q).astype(jnp.bfloat16)
    key_rows = dot_plain(inputs, wk).astype(jnp.bfloat16)
    values = (dot_plain(inputs, wv) + value_b * delta_v).astype(jnp.bfloat16)
    q_heads = split_heads(queries)
    k_heads = split_heads(key_rows)
    v_heads = split_heads(values)

    def attend_block(pieces):
        q_blk, k_blk, v_blk, live_keys = pieces
        scores = (
            jnp.einsum("qd,kd->qk", q_blk, k_blk, preferred_element_type=jnp.float32) * head_scale
        )
        scores = jnp.where(live_keys[None, :] > 0, scores, neg_fill)
        row_max = jnp.max(scores, axis=-1, keepdims=True)
        log_total = row_max + jnp.log(jnp.sum(jnp.exp(scores - row_max), axis=-1, keepdims=True))
        probs = jnp.exp(scores - log_total).astype(jnp.bfloat16)
        context = jnp.dot(probs, v_blk, preferred_element_type=jnp.float32).astype(jnp.bfloat16)
        return (context, log_total[:, 0])

    ctx_heads, log_totals = lax.map(attend_block, (q_heads, k_heads, v_heads, key_live))
    context = join_heads(ctx_heads)
    h_one = inputs + dot_plain(context, wo)
    x_one = layer_norm(h_one, gain_one)
    x_low = x_one.astype(jnp.bfloat16)

    def feed_block(block):
        act = exact_gelu(dot_plain(block, wu)).astype(jnp.bfloat16)
        return dot_plain(act, wd)

    x_blocks = x_low.reshape(SEQ_DEV, L, D)
    ffn_out = lax.map(feed_block, x_blocks).reshape(row_count, D)
    h_two = x_one + ffn_out
    output = layer_norm(h_two, gain_two)
    cot_rows = cotangent.reshape(row_count, D).astype(jnp.float32) * live_rows
    _, norm_two_back = jax.vjp(lambda hidden: layer_norm(hidden, gain_two), h_two)
    g_h2 = norm_two_back(cot_rows)[0]
    back_mats = (
        lax.all_gather(local_mats[0], ("dp", "fsdp"), axis=0, tiled=True),
        lax.all_gather(local_mats[1], ("dp", "fsdp"), axis=0, tiled=True),
        lax.all_gather(local_mats[2], ("dp", "fsdp"), axis=0, tiled=True),
        lax.all_gather(local_mats[3], ("dp", "fsdp"), axis=0, tiled=True),
        lax.all_gather(local_mats[4], ("dp", "fsdp"), axis=0, tiled=True),
        lax.all_gather(local_mats[5], ("dp", "fsdp"), axis=0, tiled=True),
        lax.all_gather(local_mats[6], ("dp", "fsdp"), axis=0, tiled=True),
        lax.all_gather(local_mats[7], ("dp", "fsdp"), axis=0, tiled=True),
    )
    bq_mat, bk_mat, bv_mat, bo_mat, bu_mat, bd_mat, back_a, back_b = back_mats
    g_ffn = g_h2.astype(jnp.bfloat16)

    def feed_back(pieces):
        block, grad_out = pieces
        pre_act = dot_plain(block, bu_mat)
        g_act = dot_trans(grad_out, bd_mat)
        _, gelu_back = jax.vjp(exact_gelu, pre_act)
        g_pre = gelu_back(g_act)[0].astype(jnp.bfloat16)
        return dot_trans(g_pre, bu_mat)

    g_x1 = g_h2 + lax.map(feed_back, (x_blocks, g_ffn.reshape(SEQ_DEV, L, D))).reshape(row_count, D)
    _, norm_one_back = jax.vjp(lambda hidden: layer_norm(hidden, gain_one), h_one)
    g_h1 = norm_one_back(g_x1)[0]
    g_attn = g_h1.astype(jnp.bfloat16)
    g_context = dot_trans(g_attn, bo_mat).astype(jnp.bfloat16)
    gc_heads = split_heads(g_context)

    def attend_back(pieces):
        q_blk, k_blk, v_blk, live_keys, log_total, gc_blk = pieces
        scores = (
            jnp.einsum("qd,kd->qk", q_blk, k_blk, preferred_element_type=jnp.float32) * head_scale
        )
        scores = jnp.where(live_keys[None, :] > 0, scores, neg_fill)
        probs = jnp.exp(scores - log_total[:, None])
        probs_low = probs.astype(jnp.bfloat16)
        g_probs = jnp.einsum("qd,kd->qk", gc_blk, v_blk, preferred_element_type=jnp.float32)
        g_scores = (probs * (g_probs - jnp.sum(g_probs * probs, axis=-1, keepdims=True))).astype(
            jnp.bfloat16
        )
        g_q = (jnp.dot(g_scores, k_blk, preferred_element_type=jnp.float32) * head_scale).astype(
            jnp.bfloat16
        )
        g_k = (
            jnp.einsum("qk,qd->kd", g_scores, q_blk, preferred_element_type=jnp.float32)
            * head_scale
        ).astype(jnp.bfloat16)
        g_v = jnp.einsum("qk,qd->kd", probs_low, gc_blk, preferred_element_type=jnp.float32).astype(
            jnp.bfloat16
        )
        return (g_q, g_k, g_v)

    gq_heads, gk_heads, gv_heads = lax.map(
        attend_back, (q_heads, k_heads, v_heads, key_live, log_totals, gc_heads)
    )
    g_queries = join_heads(gq_heads)
    g_keys = join_heads(gk_heads)
    g_values = join_heads(gv_heads)
    gq_wide = g_queries.astype(jnp.float32)
    gv_wide = g_values.astype(jnp.float32)
    grad_qb = jnp.sum(gq_wide * delta_q, axis=0)
    grad_vb = jnp.sum(gv_wide * delta_v, axis=0)
    g_dq = (query_b * gq_wide).astype(jnp.bfloat16)
    g_dv = (value_b * gv_wide).astype(jnp.bfloat16)
    t_q = dot_trans(g_dq, back_b)
    t_v = dot_trans(g_dv, back_b)
    grad_qd = jnp.sum(t_q * rank_act, axis=0)
    grad_vd = jnp.sum(t_v * rank_act, axis=0)
    g_rank = (t_q * query_d + t_v * value_d).astype(jnp.bfloat16)
    g_inputs = (
        g_h1
        + dot_trans(g_queries, bq_mat)
        + dot_trans(g_keys, bk_mat)
        + dot_trans(g_values, bv_mat)
        + dot_trans(g_rank, back_a)
    )
    sum_qd, sum_qb, sum_vd, sum_vb = lax.psum((grad_qd, grad_qb, grad_vd, grad_vb), ("dp", "fsdp"))
    rank_stats = total_square / total_count
    output_out = output.astype(jnp.bfloat16).reshape(SEQ_DEV, L, D)
    grad_tokens = g_inputs.astype(jnp.bfloat16).reshape(SEQ_DEV, L, D)
    return (output_out, grad_tokens, sum_qd, sum_qb, sum_vd, sum_vb, rank_stats)


def solution(mesh):
    in_specs = (
        P(("dp", "fsdp"), None, None),
        P(("dp", "fsdp")),
        P(("dp", "fsdp"), None, None),
        P(("dp", "fsdp"), None),
        P(("dp", "fsdp"), None),
        P(("dp", "fsdp"), None),
        P(("dp", "fsdp"), None),
        P(("dp", "fsdp"), None),
        P(("dp", "fsdp"), None),
        P(("dp", "fsdp"), None),
        P(("dp", "fsdp"), None),
        P(),
        P(),
        P(),
        P(),
        P(),
        P(),
    )
    out_specs = (
        P(("dp", "fsdp"), None, None),
        P(("dp", "fsdp"), None, None),
        P(),
        P(),
        P(),
        P(),
        P(),
    )
    return jax.shard_map(shards, mesh=mesh, in_specs=in_specs, out_specs=out_specs, check_vma=False)
```

profile of v0, /device:TPU:0, one launch (start us, length us, event | category | flops | bytes accessed | tf_op | source)
XLA Modules:
  0.0 919.7 jit_solution(1533905239916311515)
XLA Ops:
  15.9 51.6 %all-gather.15.cloned.1.call-done = bf16[768,768]{1,0:T(8,128)(2,1)} async-done(((bf16[24,768]{1,0:T(8,128)(2,1)}), bf16[768,768]{1,0:T(8,128)(2,1)}) %all-gather.15.cloned.1.call-update) | async-done | bytes 1179664 | tf_op jit(solution)/shard_map/all_gather | solution.py:68
  67.5 3.1 convolution_convert_fusion.3
  72.6 3.5 copy.62
  76.1 48.2 %all-gather.11.cloned.1.call-done = bf16[768,1024]{1,0:T(8,128)(2,1)} async-done(((bf16[24,1024]{1,0:T(8,128)(2,1)}), bf16[768,1024]{1,0:T(8,128)(2,1)}) %all-gather.11.cloned.1.call-update) | async-done | bytes 1572880 | tf_op jit(solution)/shard_map/all_gather | solution.py:73
  124.3 5.1 fusion.191
  129.5 51.7 %all-gather.13.cloned.1.call-done = bf16[1024,768]{1,0:T(8,128)(2,1)} async-done(((bf16[32,768]{1,0:T(8,128)(2,1)}), bf16[1024,768]{1,0:T(8,128)(2,1)}) %all-gather.13.cloned.1.call-update) | async-done | bytes 1572880 | tf_op jit(solution)/shard_map/all_gather | solution.py:74
  181.1 4.5 fusion.169
  185.6 51.1 %all-gather.9.cloned.1.call-done = bf16[768,768]{1,0:T(8,128)(2,1)} async-done(((bf16[24,768]{1,0:T(8,128)(2,1)}), bf16[768,768]{1,0:T(8,128)(2,1)}) %all-gather.9.cloned.1.call-update) | async-done | bytes 1179664 | tf_op jit(solution)/shard_map/all_gather | solution.py:67
  236.7 4.3 add_convert_fusion.3
  243.9 3.4 copy.61
  247.4 4.5 fusion.170
  251.9 40.4 %all-gather.17.cloned.1.call-done = bf16[768,768]{1,0:T(8,128)(2,1)} async-done(((bf16[24,768]{1,0:T(8,128)(2,1)}), bf16[768,768]{1,0:T(8,128)(2,1)}) %all-gather.17.cloned.1.call-update) | async-done | bytes 1179664 | tf_op jit(solution)/shard_map/all_gather | solution.py:69
  292.3 4.3 add_convert_fusion.2
  298.3 2.4 reshape.197
  300.7 4.1 copy.63
  306.1 91.2 %while.46 = (s32[]{:T(128)}, bf16[24,512,64]{1,2,0:T(8,128)(2,1)}, f32[24,512]{1,0:T(8,128)}, f32[24,512]{1,0:T(8,128)S(1)}, bf16[24,512,64]{2,1,0:T(8,128)(2,1)...) while((s32[]{:T(128)}, bf16[24,512,64]{1,2,0:T(8,128)(2,1)}, ...), condition=%wide.region_3.0_spmd, body=%wide.region_0.3_spmd.sunk | while | flops 68976640 | bytes 3628133 | solution.py:109
  397.3 4.2 copy.49
  403.1 3.8 fusion.190
  410.8 2.6 all-gather.21.cloned.1.call-done
  413.3 64.7 %all-gather.23.cloned.1.call-done = bf16[3072,768]{1,0:T(8,128)(2,1)} async-done(((bf16[96,768]{1,0:T(8,128)(2,1)}), bf16[3072,768]{1,0:T(8,128)(2,1)}) %all-gather.23.cloned.1.call-update) | async-done | bytes 4718608 | tf_op jit(solution)/shard_map/all_gather | solution.py:72
  479.9 44.2 %while.47 = (s32[]{:T(128)}, f32[2,512,768]{2,1,0:T(8,128)}, bf16[2,512,768]{2,1,0:T(8,128)(2,1)}, bf16[768,3072]{1,0:T(8,128)(2,1)}, bf16[3072,768]{1,0:T(8,128)(2,1)}, /*index=5*/s32[]{:T(128)}) while((s32[]{:T(128)}, f32[2,512,768]{2,1,0:T(8,128)}, bf16[2,512,768]{2,1,0:T(8,128)(2,1)}, bf16[768,3072]{1,0:T(8,128)(2,1)}, ...), condition=%wide.region_7.8_spmd, body=%wide.region_6.7_spmd.sunk | while | flops 4934074368 | bytes 11797573 | solution.py:120
  479.9 22.0 %bitcast_dynamic-update-slice_fusion.4 = f32[2,512,768]{2,1,0:T(8,128)} fusion(f32[2,512,768]{2,1,0:T(8,128)} %get-tuple-element.483, s32[]{:T(128)} %get-tuple-element.482, bf16[3072,768]{1,0:T(8,128)(2,1)} %get-tuple-element.492, bf16[768,3072]{1,0:T(8,128)(2,1)} %get-tuple-element.491, bf16[2,512,768]{2,1,0:T(8,128)(2,1)} %get-tuple-element.490), kind=kOutput, calls=%fused_computation.20.clone.1 | convolution fusion | flops 4934074368 | bytes 11797504 | tf_op jit(solution)/shard_map/while/body/eval_jaxpr/dot_general | solution.py:27
  501.9 21.8 %bitcast_dynamic-update-slice_fusion.4 = f32[2,512,768]{2,1,0:T(8,128)} fusion(f32[2,512,768]{2,1,0:T(8,128)} %get-tuple-element.483, s32[]{:T(128)} %get-tuple-element.482, bf16[3072,768]{1,0:T(8,128)(2,1)} %get-tuple-element.492, bf16[768,3072]{1,0:T(8,128)(2,1)} %get-tuple-element.491, bf16[2,512,768]{2,1,0:T(8,128)(2,1)} %get-tuple-element.490), kind=kOutput, calls=%fused_computation.20.clone.1 | convolution fusion | flops 4934074368 | bytes 11797504 | tf_op jit(solution)/shard_map/while/body/eval_jaxpr/dot_general | solution.py:27
  524.2 2.8 fusion.188
  528.4 2.8 fusion.187
  532.8 1.8 broadcast.294
  534.7 67.9 %while.48 = (s32[]{:T(128)}, f32[2,512,768]{2,1,0:T(8,128)}, bf16[2,512,768]{2,1,0:T(8,128)(2,1)}, bf16[768,3072]{1,0:T(8,128)(2,1)}, bf16[2,512,768]{2,1,0:T(8,128)(2,1)}, /*index=5*/bf16[3072,768]{1,0:T(8,128)(2,1)}, s32[]{:T(128)}) while((s32[]{:T(128)}, f32[2,512,768]{2,1,0:T(8,128)}, bf16[2,512,768]{2,1,0:T(8,128)(2,1)}, ...), condition=%wide.region_13.14_spmd, body=%wide.region_12.13_spmd.sunk | while | flops 7361003520 | bytes 29886028 | solution.py:147
  537.2 7.8 fusion.262
  545.1 24.7 %bitcast_dynamic-update-slice_fusion.5 = f32[2,512,768]{2,1,0:T(8,128)} fusion(f32[2,512,768]{2,1,0:T(8,128)} %get-tuple-element.502, s32[]{:T(128)} %get-tuple-element.501, bf16[768,3072]{1,0:T(8,128)(2,1)} %get-tuple-element.511, f32[512,3072]{1,0:T(8,128)} %fusion.262, bf16[3072,768]{1,0:T(8,128)(2,1)} %get-tuple-element.513, ...), kind=kOutput, calls=%fused_computation.77.clone.1 | convolution fusion | flops 4945084416 | bytes 18088960 | tf_op jit(solution)/shard_map/while/body/eval_jaxpr/dot_general | solution.py:31
  569.7 7.8 fusion.262
  577.6 24.6 %bitcast_dynamic-update-slice_fusion.5 = f32[2,512,768]{2,1,0:T(8,128)} fusion(f32[2,512,768]{2,1,0:T(8,128)} %get-tuple-element.502, s32[]{:T(128)} %get-tuple-element.501, bf16[768,3072]{1,0:T(8,128)(2,1)} %get-tuple-element.511, f32[512,3072]{1,0:T(8,128)} %fusion.262, bf16[3072,768]{1,0:T(8,128)(2,1)} %get-tuple-element.513, ...), kind=kOutput, calls=%fused_computation.77.clone.1 | convolution fusion | flops 4945084416 | bytes 18088960 | tf_op jit(solution)/shard_map/while/body/eval_jaxpr/dot_general | solution.py:31
  602.6 4.0 multiply_reduce_fusion.4
  607.3 1.8 fusion.186
  613.0 2.4 reshape.206
  615.4 4.1 copy.66
  623.6 211.6 %while.49 = (s32[]{:T(128)}, bf16[24,512,64]{1,2,0:T(8,128)(2,1)}, bf16[24,512,64]{1,2,0:T(8,128)(2,1)}, bf16[24,512,64]{1,2,0:T(8,128)(2,1)}, f32[24,512]{1,0:T...) while((s32[]{:T(128)}, bf16[24,512,64]{1,2,0:T(8,128)(2,1)}, ...), condition=%wide.region_18.19_spmd, body=%wide.region_16.18_spmd.sunk | while | flops 170295296 | bytes 8996981 | solution.py:178
  689.6 1.9 fusion.273
  733.7 1.8 fusion.273
  830.7 1.8 fusion.273
  835.2 3.0 copy.56
  840.4 3.0 copy.58
  844.6 3.2 copy.57
  849.4 2.8 fusion.160
  854.4 3.9 multiply_reduce_fusion.1
  858.3 39.8 %all-reduce = (f32[1024]{0:T(1024)}, f32[768]{0:T(1024)}, f32[1024]{0:T(1024)}, f32[768]{0:T(1024)}, f32[1024]{0:T(1024)S(1)}, /*index=5*/f32[]{:T(128)}) all-reduce(f32[1024]{0:T(1024)S(1)} %get-tuple-element.184, f32[768]{0:T(1024)S(1)} %get-tuple-element.267, ...), channel_id=1, replica_groups=mesh['dp'=8,'fsdp'=4] {'dp','fsdp'}, use_global_device_ids=true, to_apply=%region_20.21 | all-reduce | flops 4609 | bytes 36872 | tf_op jit(solution)/shard_map/psum | solution.py:202
  899.3 3.3 fusion.192
  903.6 3.4 fusion.171
  909.3 3.4 add_convert_fusion.1
  (488 shorter events, 342.6 us)
Async XLA Ops:
  7.2 60.3 %all-gather.15.cloned.1.call-start = ((), (), s32[]{:S(2)}) async-start(), calls=%async_computation.3 | async-start | bytes 1216512 | tf_op jit(solution)/shard_map/all_gather | solution.py:68
  7.9 116.4 %all-gather.11.cloned.1.call-start = ((), (), s32[]{:S(2)}) async-start(), calls=%async_computation.1 | async-start | bytes 1622016 | tf_op jit(solution)/shard_map/all_gather | solution.py:73
  8.6 172.5 %all-gather.13.cloned.1.call-start = ((), (), s32[]{:S(2)}) async-start(), calls=%async_computation.2 | async-start | bytes 1622016 | tf_op jit(solution)/shard_map/all_gather | solution.py:74
  9.4 227.4 %all-gather.9.cloned.1.call-start = ((), (), s32[]{:S(2)}) async-start(), calls=%async_computation | async-start | bytes 1216512 | tf_op jit(solution)/shard_map/all_gather | solution.py:67
  10.0 282.4 %all-gather.17.cloned.1.call-start = ((), (), s32[]{:S(2)}) async-start(), calls=%async_computation.4 | async-start | bytes 1216512 | tf_op jit(solution)/shard_map/all_gather | solution.py:69
  10.5 392.5 %all-gather.19.cloned.1.call-start = ((), (), s32[]{:S(2)}) async-start(), calls=%async_computation.5 | async-start | bytes 1216512 | tf_op jit(solution)/shard_map/all_gather | solution.py:70
  11.1 402.2 %all-gather.21.cloned.1.call-start = ((), (), s32[]{:S(2)}) async-start(), calls=%async_computation.6 | async-start | bytes 4866048 | tf_op jit(solution)/shard_map/all_gather | solution.py:71
  11.9 466.2 %all-gather.23.cloned.1.call-start = ((), (), s32[]{:S(2)}) async-start(), calls=%async_computation.7 | async-start | bytes 4866048 | tf_op jit(solution)/shard_map/all_gather | solution.py:72
  72.6 51.7 %copy-start.45 = (bf16[2,512,768]{2,1,0:T(8,128)(2,1)S(1)}, bf16[2,512,768]{2,1,0:T(8,128)(2,1)}, u32[]{:S(2)}) copy-start(bf16[2,512,768]{2,1,0:T(8,128)(2,1)} %param.25) | copy-start | bytes 4718596
  76.1 105.0 %copy-start.41 = (f32[1024]{0:T(1024)S(1)}, f32[1024]{0:T(1024)}, u32[]{:S(2)}) copy-start(f32[1024]{0:T(1024)} %param.38) | copy-start | bytes 12292
  129.5 107.3 %copy-start.48 = (f32[768]{0:T(1024)S(1)}, f32[768]{0:T(1024)}, u32[]{:S(2)}) copy-start(f32[768]{0:T(1024)} %param.39) | copy-start | bytes 9220
  185.6 51.1 %copy-start.16 = (f32[1024,768]{1,0:T(8,128)}, f32[1024,768]{1,0:T(8,128)S(1)}, u32[]{:S(2)}) copy-start(f32[1024,768]{1,0:T(8,128)S(1)} %fusion.169) | copy-start | bytes 9437188
  243.9 3.5 copy-start.43
  247.4 44.9 %copy-start.39 = (f32[768]{0:T(1024)S(1)}, f32[768]{0:T(1024)}, u32[]{:S(2)}) copy-start(f32[768]{0:T(1024)} %param.41) | copy-start | bytes 9220
  251.9 40.5 %copy-start.18 = (f32[1024,768]{1,0:T(8,128)}, f32[1024,768]{1,0:T(8,128)S(1)}, u32[]{:S(2)}) copy-start(f32[1024,768]{1,0:T(8,128)S(1)} %fusion.170) | copy-start | bytes 9437188
  397.3 5.8 copy-start.11
  397.3 5.8 copy-start.25
  406.9 2.2 copy-start.26
  479.9 44.2 %copy-start.1 = (f32[1024,768]{1,0:T(8,128)S(1)}, f32[1024,768]{1,0:T(8,128)}, u32[]{:S(2)}) copy-start(f32[1024,768]{1,0:T(8,128)} %copy-done) | copy-start | bytes 9437188
  479.9 44.2 %copy-start.23 = (f32[1024]{0:T(1024)S(1)}, f32[1024]{0:T(1024)}, u32[]{:S(2)}) copy-start(f32[1024]{0:T(1024)} %copy-done.22) | copy-start | bytes 12292
  479.9 44.2 %copy-start.27 = (f32[768]{0:T(1024)S(1)}, f32[768]{0:T(1024)}, u32[]{:S(2)}) copy-start(f32[768]{0:T(1024)} %param.36) | copy-start | bytes 9220
  479.9 44.2 %copy-start.32 = (f32[1024]{0:T(1024)S(1)}, f32[1024]{0:T(1024)}, u32[]{:S(2)}) copy-start(f32[1024]{0:T(1024)} %copy-done.31) | copy-start | bytes 12292
  524.1 2.8 copy-start.14
  524.2 2.8 copy-start.29
  524.2 2.8 copy-start.38
  531.2 3.4 copy-start.3
  531.2 3.4 copy-start.34
  534.6 67.9 %copy-start.2 = (f32[1024,768]{1,0:T(8,128)S(1)}, f32[1024,768]{1,0:T(8,128)}, u32[]{:S(2)}) copy-start(f32[1024,768]{1,0:T(8,128)} %copy-done) | copy-start | bytes 9437188
  534.6 67.9 %copy-start.24 = (f32[1024]{0:T(1024)S(1)}, f32[1024]{0:T(1024)}, u32[]{:S(2)}) copy-start(f32[1024]{0:T(1024)} %copy-done.22) | copy-start | bytes 12292
  534.6 67.9 %copy-start.28 = (f32[768]{0:T(1024)S(1)}, f32[768]{0:T(1024)}, u32[]{:S(2)}) copy-start(f32[768]{0:T(1024)} %param.36) | copy-start | bytes 9220
  534.6 67.9 %copy-start.35 = (f32[1024]{0:T(1024)S(1)}, f32[1024]{0:T(1024)}, u32[]{:S(2)}) copy-start(f32[1024]{0:T(1024)} %copy-done.34) | copy-start | bytes 12292
  602.6 4.0 copy-start.37
  602.6 4.0 copy-start.4
  602.6 4.7 copy-start.5
  602.6 4.7 copy-start.33
  607.3 3.5 copy-start.47
  838.6 4.8 copy-start.12
  844.5 4.9 copy-start.13
  844.6 4.9 copy-start.17
  849.4 2.8 copy-start.19
  849.4 2.8 copy-start.49
  854.4 3.9 copy-start.6
  899.3 3.4 copy-start.7
  899.3 4.3 copy-start.8
  899.3 4.3 copy-start.42
  899.3 4.3 copy-start.44
  903.6 3.4 copy-start.20
  903.6 3.5 copy-start.46
  (10 other events, 16.8 us)
Sparse Core Ops, SparseCore 0:
  10.8 56.6 all-gather.14
  70.4 53.8 all-gather.10
  127.2 53.8 all-gather.12
  183.8 52.8 all-gather.8
  239.4 52.8 all-gather.16
  295.0 52.9 all-gather.18
  350.8 62.4 all-gather.20
  416.1 61.9 all-gather.22
where the time goes:
time: 935 us; the launch traced here: 920 us
  matrix products  380 us (41%)
  waiting for transfers between devices  315 us (34%)
  local copies, waits for them, and re-layouts  112 us (12%)
  other arithmetic  52 us (6%)
  blocking collectives  39.8 us (4%)
  between operations  15.6 us (2%)
    dot_general x11, matrix products, dot_plain(): return jnp.dot(left, right, preferred_element_type=jnp.float32)  89.1 us
    dot_general x9, matrix products, dot_trans(): lax.dot_general(left, right, (((1,), (1,)), ((), ())), preferred_element_...  68.1 us
    all_gather x1, waiting for transfers between devices, shards(): lax.all_gather(local_mats[5], ('dp', 'fsdp'), axis=0, tiled=True)  64.7 us
    all_gather x1, waiting for transfers between devices, shards(): lax.all_gather(local_mats[7], ('dp', 'fsdp'), axis=0, tiled=True)  51.7 us
    all_gather x1, waiting for transfers between devices, shards(): lax.all_gather(local_mats[1], ('dp', 'fsdp'), axis=0, tiled=True)  51.6 us
    all_gather x1, waiting for transfers between devices, shards(): lax.all_gather(local_mats[0], ('dp', 'fsdp'), axis=0, tiled=True)  51.1 us
    all_gather x1, waiting for transfers between devices, shards(): lax.all_gather(local_mats[6], ('dp', 'fsdp'), axis=0, tiled=True)  48.2 us
    dot_general x24, matrix products, attend_back(): jnp.einsum('qk,qd->kd', g_scores, q_blk, preferred_element_type=jnp.float32)  43.9 us
  transfers between devices with their start and end apart: 8, of which 7 were waited for; matrix products, arithmetic and copies ran while one was open for 17% of the time, Pallas kernels for 0%

commit v1 on v0

--- a/solution.py
+++ b/solution.py
@@ -10,6 +10,18 @@
 SEQ_DEV = 2
 eps_norm = 1e-05
 neg_fill = -1000000000.0
+
+
+def doubled_up(value, axis, dim):
+    ways, here, step = (lax.axis_size(axis), lax.axis_index(axis), value.shape[dim])
+    line, have = (value, 1)
+    while have < ways:
+        line = jnp.concatenate(
+            [line, lax.ppermute(line, axis, [(d, (d - have) % ways) for d in range(ways)])],
+            axis=dim,
+        )
+        have = 2 * have
+    return jnp.roll(line, here * step, axis=dim)
 
 
 def layer_norm(hidden, gain):
@@ -70,7 +82,7 @@
         lax.all_gather(local_mats[3], ("dp", "fsdp"), axis=0, tiled=True),
         lax.all_gather(local_mats[4], ("dp", "fsdp"), axis=0, tiled=True),
         lax.all_gather(local_mats[5], ("dp", "fsdp"), axis=0, tiled=True),
-        lax.all_gather(local_mats[6], ("dp", "fsdp"), axis=0, tiled=True),
+        doubled_up(local_mats[6], ("dp", "fsdp"), 0),
         lax.all_gather(local_mats[7], ("dp", "fsdp"), axis=0, tiled=True),
     )
     wq, wk, wv, wo, wu, wd, mat_a, mat_b = full_mats

time: 935 us -> 889 us (0.951)
  waiting for transfers between devices: 315 us -> 236 us
  local copies, waits for them, and re-layouts: 112 us -> 130 us
    all_gather x1, waiting for transfers between devices: 51.6 us -> 0.01 us  [shards(): lax.all_gather(local_mats[1], ('dp', 'fsdp'), axis=0, tiled=True)]
    all_gather x1, waiting for transfers between devices: 48.2 us -> 0.01 us  [shards(): lax.all_gather(local_mats[6], ('dp', 'fsdp'), axis=0, tiled=True)]
    ppermute x0 -> x5, waiting for transfers between devices: none -> 39.7 us  [doubled_up(): lax.ppermute(line, axis, [(d, (d - have) % ways) for d in range(ways)])]
    all_gather x1, waiting for transfers between devices: 51.1 us -> 36.9 us  [shards(): lax.all_gather(local_mats[0], ('dp', 'fsdp'), axis=0, tiled=True)]
    all_gather x1, waiting for transfers between devices: 40.4 us -> 51.3 us  [shards(): lax.all_gather(local_mats[2], ('dp', 'fsdp'), axis=0, tiled=True)]
    all_gather x1, waiting for transfers between devices: 51.7 us -> 41.1 us  [shards(): lax.all_gather(local_mats[7], ('dp', 'fsdp'), axis=0, tiled=True)]
    unnamed x105 -> x121, local copies, waits for them, and re-layouts: 10.8 us -> 21.2 us
  transfers between devices with their start and end apart: 8 -> 13, of which waited for: 7 -> 9; matrix products, arithmetic and copies ran while one was open for 17% -> 63% of each run, Pallas kernels for 0% -> 0%
where the time goes in v1:
time: 889 us; the launch traced here: 873 us
  matrix products  388 us (44%)
  waiting for transfers between devices  236 us (27%)
  local copies, waits for them, and re-layouts  130 us (15%)
  other arithmetic  51.2 us (6%)
  blocking collectives  39.8 us (4%)
  between operations  15.9 us (2%)
    dot_general x11, matrix products, dot_plain(): return jnp.dot(left, right, preferred_element_type=jnp.float32)  91.6 us
    dot_general x9, matrix products, dot_trans(): lax.dot_general(left, right, (((1,), (1,)), ((), ())), preferred_element_...  74 us
    all_gather x1, waiting for transfers between devices, shards(): lax.all_gather(local_mats[5], ('dp', 'fsdp'), axis=0, tiled=True)  62.5 us
    all_gather x1, waiting for transfers between devices, shards(): lax.all_gather(local_mats[2], ('dp', 'fsdp'), axis=0, tiled=True)  51.3 us
    dot_general x24, matrix products, attend_back(): jnp.einsum('qk,qd->kd', g_scores, q_blk, preferred_element_type=jnp.float32)  43.7 us
    dot_general x24, matrix products, attend_back(): jnp.dot(g_scores, k_blk, preferred_element_type=jnp.float32) * head_scale  42.7 us
    all_gather x1, waiting for transfers between devices, shards(): lax.all_gather(local_mats[7], ('dp', 'fsdp'), axis=0, tiled=True)  41.1 us
    psum x1, blocking collectives, shards(): lax.psum((grad_qd, grad_qb, grad_vd, grad_vb), ('dp', 'fsdp'))  39.8 us
  transfers between devices with their start and end apart: 13, of which 9 were waited for; matrix products, arithmetic and copies ran while one was open for 63% of the time, Pallas kernels for 0%

profile of v1, /device:TPU:0, one launch (start us, length us, event | category | flops | bytes accessed | tf_op | source)
XLA Modules:
  0.0 873.0 jit_solution(581572281347322326)
XLA Ops:
  11.9 6.5 collective-permute-start
  18.4 2.1 collective-permute-done
  21.3 7.0 collective-permute-done.1
  29.3 3.2 collective-permute-done.2
  36.7 9.3 %collective-permute-done.3 = bf16[192,1024]{1,0:T(8,128)(2,1)S(1)} collective-permute-done((bf16[192,1024]{1,0:T(8,128)(2,1)S(1)}, bf16[192,1024]{1,0:T(8,128)(2,1)S(1)}, u32[]{:S(2)}, u32[]{:S(2)}) %collective-permute-start.3) | collective-permute-done | bytes 393248 | tf_op jit(solution)/shard_map/ppermute | solution.py:20
  50.5 18.1 %collective-permute-done.4 = bf16[384,1024]{1,0:T(8,128)(2,1)S(1)} collective-permute-done((bf16[384,1024]{1,0:T(8,128)(2,1)S(1)}, bf16[384,1024]{1,0:T(8,128)(2,1)S(1)}, u32[]{:S(2)}, u32[]{:S(2)}) %collective-permute-start.4) | collective-permute-done | bytes 786464 | tf_op jit(solution)/shard_map/ppermute | solution.py:20
  73.8 5.3 fusion.190
  79.1 2.7 convolution_convert_fusion.3
  83.8 3.5 copy.62
  87.2 41.1 %all-gather.11.cloned.1.call-done = bf16[1024,768]{1,0:T(8,128)(2,1)} async-done(((bf16[32,768]{1,0:T(8,128)(2,1)}), bf16[1024,768]{1,0:T(8,128)(2,1)}) %all-gather.11.cloned.1.call-update) | async-done | bytes 1572880 | tf_op jit(solution)/shard_map/all_gather | solution.py:86
  128.3 4.5 fusion.176
  132.8 51.3 %all-gather.15.cloned.1.call-done = bf16[768,768]{1,0:T(8,128)(2,1)} async-done(((bf16[24,768]{1,0:T(8,128)(2,1)}), bf16[768,768]{1,0:T(8,128)(2,1)}) %all-gather.15.cloned.1.call-update) | async-done | bytes 1179664 | tf_op jit(solution)/shard_map/all_gather | solution.py:81
  184.1 4.3 add_convert_fusion.2
  190.1 2.4 reshape.197
  192.4 4.1 copy.63
  196.6 6.2 fusion.178
  202.7 36.9 %all-gather.9.cloned.1.call-done = bf16[768,768]{1,0:T(8,128)(2,1)} async-done(((bf16[24,768]{1,0:T(8,128)(2,1)}), bf16[768,768]{1,0:T(8,128)(2,1)}) %all-gather.9.cloned.1.call-update) | async-done | bytes 1179664 | tf_op jit(solution)/shard_map/all_gather | solution.py:79
  239.7 5.3 add_convert_fusion.3
  244.9 2.6 copy.40
  247.5 3.8 reshape.193
  251.3 5.4 copy.61
  258.0 91.2 %while.46 = (s32[]{:T(128)}, bf16[24,512,64]{1,2,0:T(8,128)(2,1)}, f32[24,512]{1,0:T(8,128)}, f32[24,512]{1,0:T(8,128)S(1)}, bf16[24,512,64]{2,1,0:T(8,128)(2,1)...) while((s32[]{:T(128)}, bf16[24,512,64]{1,2,0:T(8,128)(2,1)}, ...), condition=%wide.region_3.4_spmd, body=%wide.region_0.3_spmd.sunk | while | flops 68976640 | bytes 3628133 | solution.py:121
  349.3 4.2 copy.49
  355.1 3.8 fusion.201
  362.7 62.5 %all-gather.21.cloned.1.call-done = bf16[3072,768]{1,0:T(8,128)(2,1)} async-done(((bf16[96,768]{1,0:T(8,128)(2,1)}), bf16[3072,768]{1,0:T(8,128)(2,1)}) %all-gather.21.cloned.1.call-update) | async-done | bytes 4718608 | tf_op jit(solution)/shard_map/all_gather | solution.py:84
  427.1 44.0 %while.47 = (s32[]{:T(128)}, f32[2,512,768]{2,1,0:T(8,128)}, bf16[2,512,768]{2,1,0:T(8,128)(2,1)}, bf16[768,3072]{1,0:T(8,128)(2,1)}, bf16[3072,768]{1,0:T(8,128)(2,1)}, /*index=5*/s32[]{:T(128)}) while((s32[]{:T(128)}, f32[2,512,768]{2,1,0:T(8,128)}, bf16[2,512,768]{2,1,0:T(8,128)(2,1)}, bf16[768,3072]{1,0:T(8,128)(2,1)}, ...), condition=%wide.region_7.8_spmd, body=%wide.region_6.7_spmd.sunk | while | flops 4934074368 | bytes 11797573 | solution.py:132
  427.1 22.0 %bitcast_dynamic-update-slice_fusion.4 = f32[2,512,768]{2,1,0:T(8,128)} fusion(f32[2,512,768]{2,1,0:T(8,128)} %get-tuple-element.493, s32[]{:T(128)} %get-tuple-element.492, bf16[3072,768]{1,0:T(8,128)(2,1)} %get-tuple-element.502, bf16[768,3072]{1,0:T(8,128)(2,1)} %get-tuple-element.501, bf16[2,512,768]{2,1,0:T(8,128)(2,1)} %get-tuple-element.500), kind=kOutput, calls=%fused_computation.20.clone.1 | convolution fusion | flops 4934074368 | bytes 11797504 | tf_op jit(solution)/shard_map/while/body/eval_jaxpr/dot_general | solution.py:39
  449.1 21.9 %bitcast_dynamic-update-slice_fusion.4 = f32[2,512,768]{2,1,0:T(8,128)} fusion(f32[2,512,768]{2,1,0:T(8,128)} %get-tuple-element.493, s32[]{:T(128)} %get-tuple-element.492, bf16[3072,768]{1,0:T(8,128)(2,1)} %get-tuple-element.502, bf16[768,3072]{1,0:T(8,128)(2,1)} %get-tuple-element.501, bf16[2,512,768]{2,1,0:T(8,128)(2,1)} %get-tuple-element.500), kind=kOutput, calls=%fused_computation.20.clone.1 | convolution fusion | flops 4934074368 | bytes 11797504 | tf_op jit(solution)/shard_map/while/body/eval_jaxpr/dot_general | solution.py:39
  471.2 2.8 fusion.199
  475.4 2.8 fusion.198
  481.6 67.9 %while.48 = (s32[]{:T(128)}, f32[2,512,768]{2,1,0:T(8,128)}, bf16[2,512,768]{2,1,0:T(8,128)(2,1)}, bf16[768,3072]{1,0:T(8,128)(2,1)}, bf16[2,512,768]{2,1,0:T(8,128)(2,1)}, /*index=5*/bf16[3072,768]{1,0:T(8,128)(2,1)}, s32[]{:T(128)}) while((s32[]{:T(128)}, f32[2,512,768]{2,1,0:T(8,128)}, bf16[2,512,768]{2,1,0:T(8,128)(2,1)}, ...), condition=%wide.region_13.14_spmd, body=%wide.region_12.13_spmd.sunk | while | flops 7361003520 | bytes 29886028 | solution.py:159
  484.4 7.9 fusion.271
  492.3 24.7 %bitcast_dynamic-update-slice_fusion.5 = f32[2,512,768]{2,1,0:T(8,128)} fusion(f32[2,512,768]{2,1,0:T(8,128)} %get-tuple-element.512, s32[]{:T(128)} %get-tuple-element.511, bf16[768,3072]{1,0:T(8,128)(2,1)} %get-tuple-element.521, f32[512,3072]{1,0:T(8,128)} %fusion.271, bf16[3072,768]{1,0:T(8,128)(2,1)} %get-tuple-element.523, ...), kind=kOutput, calls=%fused_computation.77.clone.1 | convolution fusion | flops 4945084416 | bytes 18088960 | tf_op jit(solution)/shard_map/while/body/eval_jaxpr/dot_general | solution.py:43
  517.0 7.9 fusion.271
  524.8 24.6 %bitcast_dynamic-update-slice_fusion.5 = f32[2,512,768]{2,1,0:T(8,128)} fusion(f32[2,512,768]{2,1,0:T(8,128)} %get-tuple-element.512, s32[]{:T(128)} %get-tuple-element.511, bf16[768,3072]{1,0:T(8,128)(2,1)} %get-tuple-element.521, f32[512,3072]{1,0:T(8,128)} %fusion.271, bf16[3072,768]{1,0:T(8,128)(2,1)} %get-tuple-element.523, ...), kind=kOutput, calls=%fused_computation.77.clone.1 | convolution fusion | flops 4945084416 | bytes 18088960 | tf_op jit(solution)/shard_map/while/body/eval_jaxpr/dot_general | solution.py:43
  549.7 4.0 multiply_reduce_fusion.1
  560.1 2.4 reshape.206
  562.4 4.1 copy.66
  570.6 211.2 %while.49 = (s32[]{:T(128)}, bf16[24,512,64]{1,2,0:T(8,128)(2,1)}, bf16[24,512,64]{1,2,0:T(8,128)(2,1)}, bf16[24,512,64]{1,2,0:T(8,128)(2,1)}, f32[24,512]{1,0:T...) while((s32[]{:T(128)}, bf16[24,512,64]{1,2,0:T(8,128)(2,1)}, ...), condition=%wide.region_18.19_spmd, body=%wide.region_16.18_spmd.sunk | while | flops 170295296 | bytes 8996981 | solution.py:190
  781.7 3.0 copy.56
  785.9 3.0 copy.58
  790.9 3.2 copy.57
  802.3 4.0 fusion.164
  806.3 39.8 %all-reduce = (f32[1024]{0:T(1024)}, f32[768]{0:T(1024)}, f32[1024]{0:T(1024)}, f32[768]{0:T(1024)}, f32[1024]{0:T(1024)S(1)}, /*index=5*/f32[]{:T(128)}) all-reduce(f32[1024]{0:T(1024)S(1)} %get-tuple-element.183, f32[768]{0:T(1024)S(1)} %get-tuple-element.277, ...), channel_id=1, replica_groups=mesh['dp'=8,'fsdp'=4] {'dp','fsdp'}, use_global_device_ids=true, to_apply=%region_20.21 | all-reduce | flops 4609 | bytes 36872 | tf_op jit(solution)/shard_map/psum | solution.py:214
  847.4 5.0 fusion.202
  852.4 3.1 fusion.203
  855.6 5.9 fusion.175
  862.5 3.3 add_convert_fusion.1
  (519 shorter events, 361.9 us)
Async XLA Ops:
  7.2 62.3 %copy-start.19 = (bf16[24,1024]{1,0:T(8,128)(2,1)S(1)}, bf16[24,1024]{1,0:T(8,128)(2,1)}, u32[]{:S(2)}) copy-start(bf16[24,1024]{1,0:T(8,128)(2,1)} %param.34) | copy-start | bytes 147460
  7.2 41.3 %copy-start.46 = (s32[2]{0:T(128)S(1)}, s32[2]{0:T(128)}, u32[]{:S(2)}) copy-start(s32[2]{0:T(128)} %param.26) | copy-start | bytes 28
  7.2 71.9 %all-gather.13.cloned.1.call-start = ((), (), s32[]{:S(2)}) async-start(), calls=%async_computation.2 | async-start | bytes 1216512 | tf_op jit(solution)/shard_map/all_gather | solution.py:80
  7.9 120.4 %all-gather.11.cloned.1.call-start = ((), (), s32[]{:S(2)}) async-start(), calls=%async_computation.1 | async-start | bytes 1622016 | tf_op jit(solution)/shard_map/all_gather | solution.py:86
  8.7 175.4 %all-gather.15.cloned.1.call-start = ((), (), s32[]{:S(2)}) async-start(), calls=%async_computation.3 | async-start | bytes 1216512 | tf_op jit(solution)/shard_map/all_gather | solution.py:81
  9.4 230.2 %all-gather.9.cloned.1.call-start = ((), (), s32[]{:S(2)}) async-start(), calls=%async_computation | async-start | bytes 1216512 | tf_op jit(solution)/shard_map/all_gather | solution.py:79
  10.0 345.1 %all-gather.17.cloned.1.call-start = ((), (), s32[]{:S(2)}) async-start(), calls=%async_computation.4 | async-start | bytes 1216512 | tf_op jit(solution)/shard_map/all_gather | solution.py:82
  10.6 352.1 %all-gather.19.cloned.1.call-start = ((), (), s32[]{:S(2)}) async-start(), calls=%async_computation.5 | async-start | bytes 4866048 | tf_op jit(solution)/shard_map/all_gather | solution.py:83
  11.1 414.1 %all-gather.21.cloned.1.call-start = ((), (), s32[]{:S(2)}) async-start(), calls=%async_computation.6 | async-start | bytes 4866048 | tf_op jit(solution)/shard_map/all_gather | solution.py:84
  11.9 843.7 %all-gather.23.cloned.1.call-start = ((), (), s32[]{:S(2)}) async-start(), calls=%async_computation.7 | async-start | bytes 1622016 | tf_op jit(solution)/shard_map/all_gather | solution.py:145
  11.9 8.5 collective-permute-start
  21.3 7.1 collective-permute-start.1
  29.2 3.2 collective-permute-start.2
  33.3 12.8 %collective-permute-start.3 = (bf16[192,1024]{1,0:T(8,128)(2,1)S(1)}, bf16[192,1024]{1,0:T(8,128)(2,1)S(1)}, u32[]{:S(2)}, u32[]{:S(2)}) collective-permute-start(bf16[192,1024]{1,0:T(8,128)(2,1)S(1)} %pad_maximum_fusion), channel_id=1, source_target_pairs={{0,24},{1,25},{2,26},{3,27},{4,28},{5,29},{6,30},{7,31},{8,0},{9,1... | collective-permute-start | bytes 1179656 | tf_op jit(solution)/shard_map/ppermute | solution.py:20
  46.9 21.7 %collective-permute-start.4 = (bf16[384,1024]{1,0:T(8,128)(2,1)S(1)}, bf16[384,1024]{1,0:T(8,128)(2,1)S(1)}, u32[]{:S(2)}, u32[]{:S(2)}) collective-permute-start(bf16[384,1024]{1,0:T(8,128)(2,1)S(1)} %get-tuple-element.260), channel_id=1, source_target_pairs={{0,16},{1,17},{2,18},{3,19},{4,20},{5,21},{6,22},{7,23},{8,24},{9,... | collective-permute-start | bytes 2359304 | tf_op jit(solution)/shard_map/ppermute | solution.py:20
  50.4 23.3 %copy-start.47 = (bf16[2,512,768]{2,1,0:T(8,128)(2,1)S(1)}, bf16[2,512,768]{2,1,0:T(8,128)(2,1)}, u32[]{:S(2)}) copy-start(bf16[2,512,768]{2,1,0:T(8,128)(2,1)} %param.25) | copy-start | bytes 4718596
  73.8 5.3 copy-start.48
  83.7 44.6 %copy-start.44 = (f32[1024]{0:T(1024)S(1)}, f32[1024]{0:T(1024)}, u32[]{:S(2)}) copy-start(f32[1024]{0:T(1024)} %param.40) | copy-start | bytes 12292
  87.2 96.8 %copy-start.51 = (f32[768]{0:T(1024)S(1)}, f32[768]{0:T(1024)}, u32[]{:S(2)}) copy-start(f32[768]{0:T(1024)} %param.41) | copy-start | bytes 9220
  132.8 51.3 %copy-start.16 = (f32[1024,768]{1,0:T(8,128)}, f32[1024,768]{1,0:T(8,128)S(1)}, u32[]{:S(2)}) copy-start(f32[1024,768]{1,0:T(8,128)S(1)} %fusion.176) | copy-start | bytes 9437188
  192.4 4.1 copy-start.42
  196.6 43.1 %copy-start.40 = (f32[768]{0:T(1024)S(1)}, f32[768]{0:T(1024)}, u32[]{:S(2)}) copy-start(f32[768]{0:T(1024)} %param.39) | copy-start | bytes 9220
  349.3 5.8 copy-start.9
  349.3 5.8 copy-start.26
  427.0 44.0 %copy-start.1 = (f32[1024,768]{1,0:T(8,128)S(1)}, f32[1024,768]{1,0:T(8,128)}, u32[]{:S(2)}) copy-start(f32[1024,768]{1,0:T(8,128)} %copy-done) | copy-start | bytes 9437188
  427.0 44.0 %copy-start.24 = (f32[1024]{0:T(1024)S(1)}, f32[1024]{0:T(1024)}, u32[]{:S(2)}) copy-start(f32[1024]{0:T(1024)} %copy-done.23) | copy-start | bytes 12292
  427.1 44.1 %copy-start.28 = (f32[768]{0:T(1024)S(1)}, f32[768]{0:T(1024)}, u32[]{:S(2)}) copy-start(f32[768]{0:T(1024)} %param.36) | copy-start | bytes 9220
  427.1 44.1 %copy-start.33 = (f32[1024]{0:T(1024)S(1)}, f32[1024]{0:T(1024)}, u32[]{:S(2)}) copy-start(f32[1024]{0:T(1024)} %copy-done.32) | copy-start | bytes 12292
  481.6 68.0 %copy-start.2 = (f32[1024,768]{1,0:T(8,128)S(1)}, f32[1024,768]{1,0:T(8,128)}, u32[]{:S(2)}) copy-start(f32[1024,768]{1,0:T(8,128)} %copy-done) | copy-start | bytes 9437188
  481.6 68.0 %copy-start.25 = (f32[1024]{0:T(1024)S(1)}, f32[1024]{0:T(1024)}, u32[]{:S(2)}) copy-start(f32[1024]{0:T(1024)} %copy-done.23) | copy-start | bytes 12292
  481.6 68.0 %copy-start.29 = (f32[768]{0:T(1024)S(1)}, f32[768]{0:T(1024)}, u32[]{:S(2)}) copy-start(f32[768]{0:T(1024)} %param.36) | copy-start | bytes 9220
  481.6 68.0 %copy-start.36 = (f32[1024]{0:T(1024)S(1)}, f32[1024]{0:T(1024)}, u32[]{:S(2)}) copy-start(f32[1024]{0:T(1024)} %copy-done.35) | copy-start | bytes 12292
  549.6 4.0 copy-start.38
  549.6 4.0 copy-start.4
  549.7 4.7 copy-start.5
  549.7 4.7 copy-start.34
  785.2 3.8 copy-start.10
  790.9 4.8 copy-start.11
  790.9 4.8 copy-start.20
  790.9 4.8 copy-start.52
  798.6 3.7 copy-start.31
  798.6 3.7 copy-start.41
  847.4 5.0 copy-start.21
  847.4 5.0 copy-start.49
  855.6 6.0 copy-start.8
  855.6 6.0 copy-start.14
  855.6 6.6 copy-start.15
  855.6 6.9 copy-start.22
  (18 other events, 43.9 us)
Sparse Core Ops, SparseCore 0:
  10.8 60.5 all-gather.12
  74.3 53.9 all-gather.10
  131.1 52.8 all-gather.14
  186.7 52.8 all-gather.8
  242.3 52.9 all-gather.16
  298.0 62.4 all-gather.18
  363.3 61.8 all-gather.20
  428.1 53.2 all-gather.22
